TPU v7x, 32 devices: a whole 2x2x4 slice. The times are simulated.
32 devices in a mesh: rep: 4 (over x, core), fsdp: 8 (over z, y).
Axes of the slice: x: 2, y: 2, z: 4, core: 2. Of those that a mesh axis runs over, the one named last changes fastest.
Arguments:
- inputs: bfloat16 [4, 384, 3584], P('rep', 'fsdp'), may hold values from -6 to 6
- cotangent: bfloat16 [4, 384, 3584], P('rep', 'fsdp'), may hold values from -6 to 6
- w_gate: bfloat16 [4, 3584, 14336], P('rep', None, 'fsdp'), may hold values from -6 to 6
- w_up: bfloat16 [4, 3584, 14336], P('rep', None, 'fsdp'), may hold values from -6 to 6
- w_down: bfloat16 [4, 14336, 3584], P('rep', 'fsdp'), may hold values from -6 to 6
- outer_params: float32 [14336, 3584], P('fsdp', 'rep'), may hold values from -6 to 6
- outer_moment: float32 [14336, 3584], P('fsdp', 'rep'), may hold values from -2 to 2
Outputs:
- new_gate: bfloat16 [4, 3584, 14336], P('rep', None, 'fsdp')
- new_up: bfloat16 [4, 3584, 14336], P('rep', None, 'fsdp')
- mixed_down: bfloat16 [4, 14336, 3584], P('rep', 'fsdp')
- new_outer: float32 [14336, 3584], P('fsdp', 'rep')
- new_moment: float32 [14336, 3584], P('fsdp', 'rep')
All inputs are finite; a program needn't handle non-finite values.
Results may differ from a plain program's by a relative error of at most 0.0075.
Values may be sent and summed in bfloat16 or wider, within the bound.
A program may use at most 192 MiB of HBM per device.

v0:
```python
import math

import jax
import jax.numpy as jnp
from jax import lax
from jax.sharding import PartitionSpec as P

D = 3584
FF = 14336


step_rate = 2.0
outer_rate = 0.7
moment_keep = 0.9
mix_share = 0.5


def gelu_pair(gate):
    const = math.sqrt(2.0 / math.pi)
    inner = const * (gate + 0.044715 * gate * gate * gate)
    tangent = jnp.tanh(inner)
    active = 0.5 * gate * (1.0 + tangent)
    slope = 0.5 * (1.0 + tangent) + 0.5 * gate * (1.0 - tangent * tangent) * const * (
        1.0 + 3.0 * 0.044715 * gate * gate
    )
    return (active, slope)


def contract_rows(left, right):
    return lax.dot_general(
        left, right, (((0,), (0,)), ((), ())), preferred_element_type=jnp.float32
    )


def outer_update(outer_params, outer_moment, share, replicas):
    delta = outer_params - share / replicas
    new_moment = moment_keep * outer_moment + delta
    new_outer = outer_params - outer_rate * (moment_keep * new_moment + delta)
    return (new_outer, new_moment)


def per_device(inputs, cotangent, w_gate, w_up, w_down, outer_params, outer_moment):
    scale_in = D ** (-0.5)
    scale_mid = FF ** (-0.5)
    wgate = w_gate[0]
    wupper = w_up[0]
    wdown = w_down[0]
    rows = lax.all_gather(inputs[0], "fsdp", axis=0, tiled=True)
    grads_out = lax.all_gather(cotangent[0], "fsdp", axis=0, tiled=True)
    gate = jnp.dot(rows, wgate, preferred_element_type=jnp.float32) * scale_in
    lifted = jnp.dot(rows, wupper, preferred_element_type=jnp.float32) * scale_in
    active, slope = gelu_pair(gate)
    hidden = (active * lifted).astype(jnp.bfloat16)
    back = (
        lax.dot_general(
            grads_out, wdown, (((1,), (1,)), ((), ())), preferred_element_type=jnp.float32
        )
        * scale_mid
    )
    d_gate = (back * lifted * slope).astype(jnp.bfloat16)
    d_up = (back * active).astype(jnp.bfloat16)
    g_gate = contract_rows(rows, d_gate) * scale_in
    g_up = contract_rows(rows, d_up) * scale_in
    g_down = contract_rows(hidden, grads_out) * scale_mid
    new_gate = (wgate.astype(jnp.float32) - step_rate * g_gate).astype(jnp.bfloat16)
    new_up = (wupper.astype(jnp.float32) - step_rate * g_up).astype(jnp.bfloat16)
    replicas = lax.axis_size("rep")
    local_down = wdown.astype(jnp.float32)
    share = lax.psum_scatter(
        local_down.astype(jnp.bfloat16), "rep", scatter_dimension=1, tiled=True
    ).astype(jnp.float32)
    new_outer, new_moment = outer_update(outer_params, outer_moment, share, replicas)
    outer_all = lax.all_gather(new_outer.astype(jnp.bfloat16), "rep", axis=1, tiled=True).astype(
        new_outer.dtype
    )
    after_down = local_down - step_rate * g_down
    mixed = (mix_share * after_down + (1.0 - mix_share) * outer_all).astype(jnp.bfloat16)
    return (new_gate[None], new_up[None], mixed[None], new_outer, new_moment)


def solution(mesh):
    in_specs = (
        P("rep", "fsdp", None),
        P("rep", "fsdp", None),
        P("rep", None, "fsdp"),
        P("rep", None, "fsdp"),
        P("rep", "fsdp", None),
        P("fsdp", "rep"),
        P("fsdp", "rep"),
    )
    out_specs = (
        P("rep", None, "fsdp"),
        P("rep", None, "fsdp"),
        P("rep", "fsdp", None),
        P("fsdp", "rep"),
        P("fsdp", "rep"),
    )
    return jax.shard_map(
        per_device, mesh=mesh, in_specs=in_specs, out_specs=out_specs, check_vma=False
    )
```

profile of v0, /device:TPU:0, one launch (start us, length us, event | category | flops | bytes accessed | tf_op | source)
XLA Modules:
  0.0 316.2 jit_solution(13047302315247246269)
XLA Ops:
  8.0 0.0 reduce-scatter.4.cloned.1.call-start
  8.0 18.1 %copy.20 = bf16[1792,3584]{0,1:T(8,128)(2,1)} copy(bf16[1792,3584]{1,0:T(8,128)(2,1)} %bitcast.51) | data formatting | bytes 25690112
  26.1 0.0 reduce-scatter.4.cloned.1.call-update
  26.1 0.0 all-gather.10.cloned.1.call-start
  26.2 0.5 all-gather.10.cloned.1.call-update
  26.7 0.0 all-gather.8.cloned.1.call-start
  26.7 0.5 all-gather.8.cloned.1.call-update
  27.3 0.0 all-gather.6.cloned.1.call-start
  27.3 103.0 %reduce-scatter.4.cloned.1.call-done = bf16[896,1792]{1,0:T(8,128)(2,1)} async-done(((bf16[3584,1792]{1,0:T(8,128)(2,1)}), bf16[896,1792]{1,0:T(8,128)(2,1)}) %reduce-scatter.4.cloned.1.call-update) | async-done | bytes 3211280
  130.4 4.6 %copy.21 = bf16[1792,896]{1,0:T(8,128)(2,1)S(1)} copy(bf16[1792,896]{0,1:T(8,128)(2,1)} %bitcast.52) | data formatting | bytes 6422528
  135.0 9.7 %fusion.50 = (bf16[1792,896]{1,0:T(8,128)(2,1)}, f32[1792,896]{1,0:T(8,128)}, f32[1792,896]{1,0:T(8,128)}) fusion(f32[1792,896]{1,0:T(8,128)} %param.12, bf16[1792,896]{1,0:T(8,128)(2,1)S(1)} %copy.21, f32[1792,896]{1,0:T(8,128)} %param.13), kind=kLoop, calls=%fused_computation.56 | loop fusion | flops 16056320 | bytes 32112640 | tf_op jit(solution)/shard_map/convert_element_type | solution.py:73
  144.6 0.0 all-gather.6.cloned.1.call-update
  144.6 19.2 %copy.16 = bf16[1,3584,1792]{1,2,0:T(8,128)(2,1)} copy(bf16[1,3584,1792]{2,1,0:T(8,128)(2,1)} %param.9) | data formatting | bytes 25690112 | tf_op args[2]
  163.8 18.1 %copy.17 = bf16[1,3584,1792]{1,2,0:T(8,128)(2,1)} copy(bf16[1,3584,1792]{2,1,0:T(8,128)(2,1)} %param.10) | data formatting | bytes 25690112 | tf_op args[3]
  181.9 0.0 all-gather.10.cloned.1.call-done
  181.9 0.0 copy-start.1
  181.9 11.6 %fusion.5 = f32[384,1792]{1,0:T(8,128)} fusion(bf16[1,3584,1792]{2,1,0:T(8,128)(2,1)} %param.9, bf16[1,384,3584]{2,1,0:T(8,128)(2,1)} %all-gather.10.cloned.1.call-done), kind=kOutput, calls=%fused_computation.8 | convolution fusion | flops 4932501504 | bytes 18350080 | tf_op jit(solution)/shard_map/dot_general | solution.py:50
  193.5 0.0 copy-done.1
  193.5 10.0 %fusion.10 = f32[384,1792]{1,0:T(8,128)} fusion(bf16[1,3584,1792]{2,1,0:T(8,128)(2,1)} %param.10, bf16[1,384,3584]{2,1,0:T(8,128)(2,1)S(1)} %copy-done.1), kind=kOutput, calls=%fused_computation.16 | convolution fusion | flops 4933189632 | bytes 18350080 | tf_op jit(solution)/shard_map/dot_general | solution.py:51
  203.5 0.0 all-gather.8.cloned.1.call-done
  203.5 14.8 %convolution_multiply_fusion = f32[384,1792]{1,0:T(8,128)} fusion(bf16[1,384,3584]{2,1,0:T(8,128)(2,1)} %all-gather.8.cloned.1.call-done, bf16[1,1792,3584]{2,1,0:T(8,128)(2,1)} %param.11), kind=kOutput, calls=%fused_computation.17 | convolution fusion | flops 4933189632 | bytes 18350080 | tf_op jit(solution)/shard_map/dot_general | solution.py:55
  218.3 18.2 %fusion.3 = bf16[1,3584,1792]{1,2,0:T(8,128)(2,1)} fusion(bf16[1,3584,1792]{1,2,0:T(8,128)(2,1)} %copy.16, bf16[1,384,3584]{2,1,0:T(8,128)(2,1)S(1)} %copy-done.1, f32[384,1792]{1,0:T(8,128)} %fusion.5, f32[384,1792]{1,0:T(8,128)} %convolution_multiply_fusion, f32[384,1792]{1,0:T(8,128)} %fusion.10), kind=kOutput, calls=%fused_computation.6 | convolution fusion | flops 4972642304 | bytes 36700160 | tf_op jit(solution)/shard_map/dot_general | solution.py:30
  236.5 18.0 %copy.18 = bf16[1,3584,1792]{2,1,0:T(8,128)(2,1)} copy(bf16[1,3584,1792]{1,2,0:T(8,128)(2,1)} %fusion.3) | data formatting | bytes 25690112
  254.5 15.7 %fusion.4 = bf16[1,3584,1792]{1,2,0:T(8,128)(2,1)} fusion(bf16[1,3584,1792]{1,2,0:T(8,128)(2,1)} %copy.17, bf16[1,384,3584]{2,1,0:T(8,128)(2,1)S(1)} %copy-done.1, f32[384,1792]{1,0:T(8,128)} %convolution_multiply_fusion, f32[384,1792]{1,0:T(8,128)} %fusion.5), kind=kOutput, calls=%fused_computation.7 | convolution fusion | flops 4965761024 | bytes 33947648 | tf_op jit(solution)/shard_map/dot_general | solution.py:30
  270.2 0.0 copy-start
  270.2 18.2 %copy.19 = bf16[1,3584,1792]{2,1,0:T(8,128)(2,1)} copy(bf16[1,3584,1792]{1,2,0:T(8,128)(2,1)} %fusion.4) | data formatting | bytes 25690112
  288.4 0.0 all-gather.6.cloned.1.call-done
  288.4 0.0 copy-done
  288.4 20.2 %fusion.2 = bf16[1,1792,3584]{2,1,0:T(8,128)(2,1)} fusion(bf16[1792,3584]{1,0:T(8,128)(2,1)} %all-gather.6.cloned.1.call-done, bf16[1,384,3584]{2,1,0:T(8,128)(2,1)S(1)} %copy-done, f32[384,1792]{1,0:T(8,128)} %fusion.10, f32[384,1792]{1,0:T(8,128)} %fusion.5, bf16[1,1792,3584]{2,1,0:T(8,128)(2,1)} %param.11), kind=kOutput, calls=%fused_computation.5 | convolution fusion | flops 4985028608 | bytes 46792704 | tf_op jit(solution)/shard_map/dot_general | solution.py:30
Async XLA Ops:
  8.0 122.4 %reduce-scatter.4.cloned.1.call-start = ((), (), s32[]{:S(2)}) async-start(), calls=%async_computation.4 | async-start | bytes 16056320
  26.1 155.7 %all-gather.10.cloned.1.call-start = ((), (), s32[]{:S(2)}) async-start(), calls=%async_computation.3 | async-start | bytes 3096576 | tf_op jit(solution)/shard_map/all_gather | solution.py:48
  26.7 176.8 %all-gather.8.cloned.1.call-start = ((), (), s32[]{:S(2)}) async-start(), calls=%async_computation.2 | async-start | bytes 3096576 | tf_op jit(solution)/shard_map/all_gather | solution.py:49
  27.3 261.1 %all-gather.6.cloned.1.call-start = ((), (), s32[]{:S(2)}) async-start(), calls=%async_computation.1 | async-start | bytes 16056320 | tf_op jit(solution)/shard_map/all_gather | solution.py:73
  181.9 11.6 %copy-start.1 = (bf16[1,384,3584]{2,1,0:T(8,128)(2,1)S(1)}, bf16[1,384,3584]{2,1,0:T(8,128)(2,1)}, u32[]{:S(2)}) copy-start(bf16[1,384,3584]{2,1,0:T(8,128)(2,1)} %all-gather.10.cloned.1.call-done) | copy-start | bytes 8257540
  270.2 18.2 %copy-start = (bf16[1,384,3584]{2,1,0:T(8,128)(2,1)S(1)}, bf16[1,384,3584]{2,1,0:T(8,128)(2,1)}, u32[]{:S(2)}) copy-start(bf16[1,384,3584]{2,1,0:T(8,128)(2,1)} %all-gather.8.cloned.1.call-done) | copy-start | bytes 8257540
Sparse Core Ops, SparseCore 0:
  26.2 104.0 reduce-scatter.3
Sparse Core Ops, SparseCore 1:
  28.8 58.6 all-gather.9
  89.5 54.5 all-gather.7
  145.5 82.6 all-gather.5
where the time goes:
time: 319 us; the launch traced here: 316 us
  waiting for transfers between devices  104 us (33%)
  local copies, waits for them, and re-layouts  96.1 us (30%)
  matrix products  90.5 us (28%)
  between operations  15.7 us (5%)
  other arithmetic  9.66 us (3%)
    unnamed x5, waiting for transfers between devices  104 us
    unnamed x10, local copies, waits for them, and re-layouts  96.1 us
    dot_general x3, matrix products, contract_rows(): lax.dot_general(left, right, (((0,), (0,)), ((), ())), preferred_element_...  54.1 us
    dot_general x1, matrix products, per_device(): lax.dot_general(grads_out, wdown, (((1,), (1,)), ((), ())), preferred_ele...  14.8 us
    dot_general x1, matrix products, per_device(): gate = jnp.dot(rows, wgate, preferred_element_type=jnp.float32) * scale_in  11.6 us
    dot_general x1, matrix products, per_device(): jnp.dot(rows, wupper, preferred_element_type=jnp.float32) * scale_in  10 us
    convert_element_type x1, other arithmetic, per_device(): new_outer.astype(jnp.bfloat16)  9.66 us
  transfers between devices with their start and end apart: 4, of which 1 were waited for; matrix products, arithmetic and copies ran while one was open for 50% of the time, Pallas kernels for 0%

commit v1 on v0

v1 whole, which is shorter than its diff:
```python
import functools
import math

import jax
import jax.numpy as jnp
from jax import lax
from jax.experimental import pallas as pl
from jax.experimental.pallas import tpu as pltpu
from jax.sharding import PartitionSpec as P


step_rate = 2.0
outer_rate = 0.7
moment_keep = 0.9
mix_share = 0.5

VMEM_LIMIT = 66 * 1000 * 1000
ANY = pl.BlockSpec(memory_space=pl.ANY)

take_average = outer_rate * (1.0 + moment_keep)
keep_params = 1.0 - take_average
keep_moment = -outer_rate * moment_keep * moment_keep

f32 = jnp.float32
bf16 = jnp.bfloat16


def gelu_pair(gate):
    const = math.sqrt(2.0 / math.pi)
    square = gate * gate
    tangent = jnp.tanh(const * (gate + 0.044715 * square * gate))
    half = 0.5 * (1.0 + tangent)
    active = gate * half
    slope = half + 0.5 * gate * (1.0 - tangent * tangent) * const * (1.0 + 3.0 * 0.044715 * square)
    return (active, slope)


def divide(extent, most, unit):
    for parts in range(most, 0, -1):
        if extent % (parts * unit) == 0:
            return parts
    return 1


def params(**more):
    return pltpu.CompilerParams(vmem_limit_bytes=VMEM_LIMIT, **more)


def cost(flops, moved):
    return pl.CostEstimate(flops=int(flops), bytes_accessed=int(moved), transcendentals=0)


def forward_body(scale_in, scale_mid, x_ref, c_ref, wg_ref, wu_ref, wd_ref, h_ref, dg_ref, du_ref):
    gate = jnp.dot(x_ref[...], wg_ref[...], preferred_element_type=f32) * scale_in
    lifted = jnp.dot(x_ref[...], wu_ref[...], preferred_element_type=f32) * scale_in
    back = (
        lax.dot_general(
            c_ref[...], wd_ref[...], (((1,), (1,)), ((), ())), preferred_element_type=f32
        )
        * scale_mid
    )
    active, slope = gelu_pair(gate)
    h_ref[...] = (active * lifted).T.astype(bf16)
    dg_ref[...] = (back * lifted * slope).astype(bf16)
    du_ref[...] = (back * active).astype(bf16)


def forward(rows, cots, wg, wu, wd, scale_in, scale_mid):
    tokens, d = rows.shape
    ff = wg.shape[1]
    tf = ff // divide(ff, 8, 128)
    tt = tokens // divide(tokens, max(1, tokens // 384), 128)
    grid = (ff // tf, tokens // tt)
    tok = pl.BlockSpec((tt, d), lambda i, j: (j, 0))
    col = pl.BlockSpec((d, tf), lambda i, j: (0, i))
    out = pl.BlockSpec((tt, tf), lambda i, j: (j, i))
    return pl.pallas_call(
        functools.partial(forward_body, scale_in, scale_mid),
        grid=grid,
        in_specs=[tok, tok, col, col, pl.BlockSpec((tf, d), lambda i, j: (i, 0))],
        out_specs=[pl.BlockSpec((tf, tt), lambda i, j: (i, j)), out, out],
        out_shape=[
            jax.ShapeDtypeStruct((ff, tokens), bf16),
            jax.ShapeDtypeStruct((tokens, ff), bf16),
            jax.ShapeDtypeStruct((tokens, ff), bf16),
        ],
        compiler_params=params(),
        cost_estimate=cost(6 * tokens * d * ff, 6 * d * ff + 10 * tokens * d),
        name="forward",
    )(rows, cots, wg, wu, wd)


def update_body(scale, x_ref, dg_ref, du_ref, wg_ref, wu_ref, ng_ref, nu_ref):
    for d_ref, w_ref, o_ref in ((dg_ref, wg_ref, ng_ref), (du_ref, wu_ref, nu_ref)):
        grad = jnp.dot(x_ref[...], d_ref[...], preferred_element_type=f32)
        o_ref[...] = (w_ref[...].astype(f32) - scale * grad).astype(bf16)


def update(turned, d_gate, d_up, wg, wu, scale):
    d, tokens = turned.shape
    ff = wg.shape[1]
    td = d // divide(d, 7, 128)
    weight = pl.BlockSpec((td, ff), lambda i: (i, 0))
    grads = pl.BlockSpec((tokens, ff), lambda i: (0, 0))
    return pl.pallas_call(
        functools.partial(update_body, scale),
        grid=(d // td,),
        in_specs=[pl.BlockSpec((td, tokens), lambda i: (i, 0)), grads, grads, weight, weight],
        out_specs=[weight, weight],
        out_shape=[jax.ShapeDtypeStruct(wg.shape, bf16)] * 2,
        compiler_params=params(),
        cost_estimate=cost(4 * tokens * d * ff, 8 * d * ff),
        name="update",
    )(turned, d_gate, d_up, wg, wu)


def join_body(*refs):
    blocks, (x_ref, c_ref, t_ref) = refs[:-3], refs[-3:]
    half = blocks[0].shape[0] // 2
    for i, block in enumerate(blocks):
        x_ref[i * half : (i + 1) * half, :] = block[:half, :]
        c_ref[i * half : (i + 1) * half, :] = block[half:, :]
    t_ref[...] = x_ref[...].T


def join(blocks):
    pair, d = blocks[0].shape
    tokens = len(blocks) * pair // 2
    td = d // divide(d, 7, 128)
    out = pl.BlockSpec((tokens, td), lambda i: (0, i))
    return pl.pallas_call(
        join_body,
        grid=(d // td,),
        in_specs=[pl.BlockSpec((pair, td), lambda i: (0, i))] * len(blocks),
        out_specs=[out, out, pl.BlockSpec((td, tokens), lambda i: (i, 0))],
        out_shape=[
            jax.ShapeDtypeStruct((tokens, d), bf16),
            jax.ShapeDtypeStruct((tokens, d), bf16),
            jax.ShapeDtypeStruct((d, tokens), bf16),
        ],
        compiler_params=params(),
        cost_estimate=cost(2e6, 10 * tokens * d),
        name="join",
    )(*blocks)


def pack_body(r_ref, w_ref, o_ref):
    o_ref[...] = w_ref[...]


def pack(rep, wd, chunk, unit, width):
    start, units = chunk
    return pl.pallas_call(
        pack_body,
        grid_spec=pltpu.PrefetchScalarGridSpec(
            num_scalar_prefetch=1,
            grid=(units, 2),
            in_specs=[
                pl.BlockSpec((unit, width), lambda j, i, r: (start + j, (r[0] ^ 1) ^ (2 * i)))
            ],
            out_specs=pl.BlockSpec((unit, width), lambda j, i, r: (j, i)),
        ),
        out_shape=jax.ShapeDtypeStruct((units * unit, 2 * width), bf16),
        compiler_params=params(),
        cost_estimate=cost(2e6, 8 * units * unit * width),
        name="pack",
    )(rep, wd)


def sums_body(count, r_ref, own_ref, far_ref, near_ref, p_ref, m_ref, o_ref):
    width = own_ref.shape[1]
    far = far_ref[...].astype(f32) + near_ref[:, width:].astype(f32)
    own = own_ref[...].astype(f32) + near_ref[:, :width].astype(f32)
    o_ref[:, :width] = far.astype(bf16)
    o_ref[:, width:] = (
        keep_params * p_ref[...] + keep_moment * m_ref[...] + (take_average / count) * own
    ).astype(bf16)


def row_specs(chunk, unit, width):
    start, _ = chunk
    own = pl.BlockSpec((unit, width), lambda i, r: (start + i, r[0]))
    far = pl.BlockSpec((unit, width), lambda i, r: (start + i, r[0] ^ 2))
    pair = pl.BlockSpec((unit, 2 * width), lambda i, r: (i, 0))
    state = pl.BlockSpec((unit, width), lambda i, r: (start + i, 0))
    return own, far, pair, state


def sums(rep, wd, near, op, om, chunk, unit, width, count):
    units = chunk[1]
    own, far, pair, state = row_specs(chunk, unit, width)
    return pl.pallas_call(
        functools.partial(sums_body, count),
        grid_spec=pltpu.PrefetchScalarGridSpec(
            num_scalar_prefetch=1,
            grid=(units,),
            in_specs=[own, far, pair, state, state],
            out_specs=pair,
        ),
        out_shape=jax.ShapeDtypeStruct((units * unit, 2 * width), bf16),
        compiler_params=params(),
        cost_estimate=cost(2e6, 20 * units * unit * width),
        name="sums",
    )(rep, wd, wd, near, op, om)


def outer_body(count, r_ref, own_ref, far_ref, near_ref, cross_ref, p_ref, m_ref, *rest):
    no_ref, nm_ref, pair_ref = rest[-3:]
    width = own_ref.shape[1]
    own = own_ref[...].astype(f32) + near_ref[:, :width].astype(f32)
    far = far_ref[...].astype(f32) + near_ref[:, width:].astype(f32)
    params_now = p_ref[...]
    delta = params_now - (own + cross_ref[:, :width].astype(f32)) / count
    moment = moment_keep * m_ref[...] + delta
    fresh = params_now - outer_rate * (moment_keep * moment + delta)
    nm_ref[...] = moment
    no_ref[...] = fresh
    pair_ref[:, :width] = fresh.astype(bf16)
    pair_ref[:, width:] = (
        cross_ref[:, width:].astype(f32) + (take_average / count) * far
    ).astype(bf16)


def outer(rep, wd, near, cross, op, om, before, after, chunk, unit, width, count):
    units = chunk[1]
    own, far, pair, state = row_specs(chunk, unit, width)
    return pl.pallas_call(
        functools.partial(outer_body, count),
        grid_spec=pltpu.PrefetchScalarGridSpec(
            num_scalar_prefetch=1,
            grid=(units,),
            in_specs=[own, far, pair, pair, state, state] + [ANY] * len(before + after),
            out_specs=[state, state, pair],
        ),
        out_shape=[
            jax.ShapeDtypeStruct(op.shape, f32),
            jax.ShapeDtypeStruct(op.shape, f32),
            jax.ShapeDtypeStruct((units * unit, 2 * width), bf16),
        ],
        input_output_aliases={7: 0, 8: 1} if before else {},
        compiler_params=params(),
        cost_estimate=cost(2e6, 28 * units * unit * width),
        name="outer",
    )(rep, wd, wd, near, cross, op, om, *before, *after)


def mixed_body(scale, r_ref, h_ref, c_ref, w_ref, mine_ref, theirs_ref, *rest):
    o_ref = rest[-1]
    grad = jnp.dot(h_ref[...], c_ref[...], preferred_element_type=f32)
    fresh = jnp.where(pl.program_id(0) < 2, mine_ref[...], theirs_ref[...]).astype(f32)
    after = w_ref[...].astype(f32) - scale * grad
    o_ref[...] = (mix_share * after + (1.0 - mix_share) * fresh).astype(bf16)


def mixed(rep, hidden, cots, wd, mine, theirs, before, chunk, unit, width, scale):
    start, units = chunk
    tokens = hidden.shape[1]

    def column(i, r):
        return r[0] ^ (2 * (i % 2) + i // 2)

    weight = pl.BlockSpec((unit, width), lambda i, j, r: (start + j, column(i, r)))
    return pl.pallas_call(
        functools.partial(mixed_body, scale),
        grid_spec=pltpu.PrefetchScalarGridSpec(
            num_scalar_prefetch=1,
            grid=(4, units),
            in_specs=[
                pl.BlockSpec((unit, tokens), lambda i, j, r: (start + j, 0)),
                pl.BlockSpec((tokens, width), lambda i, j, r: (0, column(i, r))),
                weight,
                pl.BlockSpec(
                    (unit, width),
                    lambda i, j, r: (jnp.where(i < 2, j, units - 1), jnp.minimum(i, 1)),
                ),
                pl.BlockSpec(
                    (unit, width),
                    lambda i, j, r: (jnp.where(i < 2, 0, j), jnp.maximum(i - 2, 0)),
                ),
            ]
            + [ANY] * len(before),
            out_specs=weight,
        ),
        out_shape=jax.ShapeDtypeStruct(wd.shape, bf16),
        input_output_aliases={6: 0} if before else {},
        compiler_params=params(),
        cost_estimate=cost(8 * tokens * units * unit * width, 24 * units * unit * width),
        name="mixed",
    )(rep, hidden, cots, wd, mine, theirs, *before)


def per_device(inputs, cotangent, w_gate, w_up, w_down, outer_params, outer_moment):
    d = w_gate.shape[1]
    shards = lax.axis_size("fsdp")
    ff = w_gate.shape[2] * shards
    scale_in = d ** (-0.5)
    scale_mid = ff ** (-0.5)
    wg, wu, wd = w_gate[0], w_up[0], w_down[0]
    count = lax.axis_size("rep")
    rep = lax.axis_index("rep").astype(jnp.int32).reshape(1)
    width = outer_params.shape[1]
    parts = divide(wd.shape[0], 8, 16)
    unit = wd.shape[0] // parts
    inner = parts - 2
    lengths = [n for n in (1, inner - inner // 2, inner // 2, 1) if n > 0]
    chunks = [(sum(lengths[:i]), n) for i, n in enumerate(lengths)]

    order = list(range(0, shards, 2)) + list(range(1, shards, 2))[::-1]
    forth = [(order[i], order[(i + 1) % shards]) for i in range(shards)]
    back = [(b, a) for a, b in forth]
    flip_core = [(i, i ^ 1) for i in range(count)]
    flip_chip = [(i, i ^ 2) for i in range(count)]

    longer, shorter = shards // 2, shards - 1 - shards // 2
    near, cross, packed, ready = [], [], [], []
    own = jnp.concatenate([inputs[0], cotangent[0]], axis=0)
    one, two = [own], [own]

    def hop(step):
        if step < longer:
            one.append(lax.ppermute(one[-1], "fsdp", forth))
        if step < shorter:
            two.append(lax.ppermute(two[-1], "fsdp", back))

    hop(0)
    for chunk in chunks:
        packed.append(pack(rep, wd, chunk, unit, width))
        near.append(lax.ppermute(packed[-1], "rep", flip_core))
    for chunk, other in zip(chunks, near):
        ready.append(sums(rep, wd, other, outer_params, outer_moment, chunk, unit, width, count))
        cross.append(lax.ppermute(ready[-1], "rep", flip_chip))
    for step in range(1, longer):
        hop(step)
    rows, cots, turned = join(one + two[:0:-1])

    hidden, d_gate, d_up = forward(rows, cots, wg, wu, wd, scale_in, scale_mid)
    new_gate, new_up = update(turned, d_gate, d_up, wg, wu, step_rate * scale_in)

    state, out = (), ()
    for k, chunk in enumerate(chunks):
        after = (hidden,) if k < 2 else (new_gate,)
        new_outer, new_moment, mine = outer(
            rep, wd, near[k], cross[k], outer_params, outer_moment, state, after, chunk,
            unit, width, count,
        )
        state = (new_outer, new_moment)
        theirs = lax.ppermute(mine, "rep", flip_core)
        out = (
            mixed(
                rep, hidden, cots, wd, mine, theirs, out, chunk, unit, width,
                step_rate * scale_mid,
            ),
        )
    return (new_gate[None], new_up[None], out[0][None], new_outer, new_moment)


def solution(mesh):
    in_specs = (
        P("rep", "fsdp", None),
        P("rep", "fsdp", None),
        P("rep", None, "fsdp"),
        P("rep", None, "fsdp"),
        P("rep", "fsdp", None),
        P("fsdp", "rep"),
        P("fsdp", "rep"),
    )
    out_specs = (
        P("rep", None, "fsdp"),
        P("rep", None, "fsdp"),
        P("rep", "fsdp", None),
        P("fsdp", "rep"),
        P("fsdp", "rep"),
    )
    return jax.shard_map(
        per_device, mesh=mesh, in_specs=in_specs, out_specs=out_specs, check_vma=False
    )
```

time: 319 us -> 294 us (0.922)
  Pallas kernels: 0 us -> 150 us
  local copies, waits for them, and re-layouts: 96.1 us -> 4.48 us
  matrix products: 90.5 us -> 0 us
  waiting for transfers between devices: 104 us -> 121 us
  between operations: 15.7 us -> 0.7 us
  starting transfers between devices: 0.16 us -> 14.7 us
  other arithmetic: 9.66 us -> 1.02 us
    pallas_call x0 -> x19, Pallas kernels: none -> 150 us  [the longest x4 36.5 us: mixed(): pl.pallas_call(functools.partial(mixed_body, scale), grid_spec=pltpu.Pref...]
    ppermute x0 -> x19, waiting for transfers between devices: none -> 121 us  [the longest x4 83.4 us: per_device(): cross.append(lax.ppermute(ready[-1], 'rep', flip_chip))]
    unnamed x5 -> x0, waiting for transfers between devices: 104 us -> none
    unnamed x10 -> x14, local copies, waits for them, and re-layouts: 96.1 us -> 4.48 us
    dot_general x6 -> x0, matrix products: 90.5 us -> none  [the longest x3 54.1 us: contract_rows(): lax.dot_general(left, right, (((0,), (0,)), ((), ())), preferred_element_...]
    ppermute x0 -> x19, starting transfers between devices: none -> 14.7 us  [the longest x4 7.16 us: hop(): one.append(lax.ppermute(one[-1], 'fsdp', forth))]
    convert_element_type x1 -> x0, other arithmetic: 9.66 us -> none  [per_device(): new_outer.astype(jnp.bfloat16)]
  transfers between devices with their start and end apart: 4 -> 19, of which waited for: 1 -> 8; matrix products, arithmetic and copies ran while one was open for 50% -> 0% of each run, Pallas kernels for 0% -> 48%
where the time goes in v1:
time: 294 us; the launch traced here: 292 us
  Pallas kernels  150 us (51%)
  waiting for transfers between devices  121 us (41%)
  starting transfers between devices  14.7 us (5%)
  local copies, waits for them, and re-layouts  4.48 us (2%)
    ppermute x4, waiting for transfers between devices, per_device(): cross.append(lax.ppermute(ready[-1], 'rep', flip_chip))  83.4 us
    pallas_call x4, Pallas kernels, mixed(): pl.pallas_call(functools.partial(mixed_body, scale), grid_spec=pltpu.Pref...  36.5 us
    ppermute x4, waiting for transfers between devices, hop(): one.append(lax.ppermute(one[-1], 'fsdp', forth))  29 us
    pallas_call x1, Pallas kernels, update(): pl.pallas_call(functools.partial(update_body, scale), grid=(d // td,), in...  25.6 us
    pallas_call x4, Pallas kernels, outer(): pl.pallas_call(functools.partial(outer_body, count), grid_spec=pltpu.Pref...  24.1 us
    pallas_call x1, Pallas kernels, forward(): pl.pallas_call(functools.partial(forward_body, scale_in, scale_mid), grid...  23.8 us
    pallas_call x4, Pallas kernels, sums(): pl.pallas_call(functools.partial(sums_body, count), grid_spec=pltpu.Prefe...  18.3 us
    pallas_call x4, Pallas kernels, pack(): pl.pallas_call(pack_body, grid_spec=pltpu.PrefetchScalarGridSpec(num_scal...  13.8 us
  transfers between devices with their start and end apart: 19, of which 8 were waited for; matrix products, arithmetic and copies ran while one was open for 0% of the time, Pallas kernels for 48%

profile of v1, /device:TPU:0, one launch (start us, length us, event | category | flops | bytes accessed | tf_op | source)
XLA Modules:
  0.0 292.1 jit_solution(17325463238341646185)
XLA Ops:
  0.6 5.0 %pack.6 = bf16[672,1792]{1,0:T(8,128)(2,1)} custom-call(s32[1]{0:T(128)} %bitcast.7.r_ref, bf16[1792,3584]{1,0:T(8,128)(2,1)} %bitcast.9), custom_call_target="tpu_custom_call" | custom-call | flops 2000000 | bytes 4816896 | tf_op jit(solution)/shard_map/pack/pallas_call | solution.py:153
  7.2 2.6 collective-permute-start
  9.8 4.9 %pack.5 = bf16[672,1792]{1,0:T(8,128)(2,1)} custom-call(s32[1]{0:T(128)} %bitcast.7.r_ref, bf16[1792,3584]{1,0:T(8,128)(2,1)} %bitcast.10), custom_call_target="tpu_custom_call" | custom-call | flops 2000000 | bytes 4816896 | tf_op jit(solution)/shard_map/pack/pallas_call | solution.py:153
  15.4 10.6 %collective-permute-done.refs_1_ = bf16[96,3584]{1,0:T(8,128)(2,1)} collective-permute-done((bf16[96,3584]{1,0:T(8,128)(2,1)S(1)}, bf16[96,3584]{1,0:T(8,128)(2,1)}, u32[]{:S(2)}, u32[]{:S(2)}) %collective-permute-start) | collective-permute-done | bytes 688160 | tf_op jit(solution)/shard_map/ppermute | solution.py:321
  26.0 1.8 collective-permute-start.1
  27.8 4.9 %collective-permute-done.4.refs_7_ = bf16[96,3584]{1,0:T(8,128)(2,1)} collective-permute-done((bf16[96,3584]{1,0:T(8,128)(2,1)S(1)}, bf16[96,3584]{1,0:T(8,128)(2,1)}, u32[]{:S(2)}, u32[]{:S(2)}) %collective-permute-start.4) | collective-permute-done | bytes 688160 | tf_op jit(solution)/shard_map/ppermute | solution.py:323
  33.0 10.6 %collective-permute-done.1.refs_2_ = bf16[96,3584]{1,0:T(8,128)(2,1)} collective-permute-done((bf16[96,3584]{1,0:T(8,128)(2,1)}, bf16[96,3584]{1,0:T(8,128)(2,1)}, u32[]{:S(2)}, u32[]{:S(2)}) %collective-permute-start.1) | collective-permute-done | bytes 688160 | tf_op jit(solution)/shard_map/ppermute | solution.py:321
  43.5 1.5 collective-permute-start.2
  45.1 6.0 %sums.6 = bf16[672,1792]{1,0:T(8,128)(2,1)} custom-call(s32[1]{0:T(128)} %bitcast.7.r_ref, bf16[1792,3584]{1,0:T(8,128)(2,1)} %bitcast.11, bf16[1792,3584]{1,0:T(8,128)(2,1)} %bitcast.12, bf16[672,1792]{1,0:T(8,128)(2,1)} %collective-permute-done.11.near_ref, f32[1792,896]{1,0:T(8,128)} %p_ref.15, f32[1792,896]{1,0:T(8,128)} %m_ref.15), custom_call_target="tpu_custom_call" | custom-call | flops 2000000 | bytes 12042240 | tf_op jit(solution)/shard_map/sums/pallas_call | solution.py:192
  51.1 1.5 collective-permute-start.12
  52.6 1.9 pack.7
  55.0 5.3 %collective-permute-done.2.refs_3_ = bf16[96,3584]{1,0:T(8,128)(2,1)} collective-permute-done((bf16[96,3584]{1,0:T(8,128)(2,1)}, bf16[96,3584]{1,0:T(8,128)(2,1)}, u32[]{:S(2)}, u32[]{:S(2)}) %collective-permute-start.2) | collective-permute-done | bytes 688160 | tf_op jit(solution)/shard_map/ppermute | solution.py:321
  61.5 6.0 %sums.5 = bf16[672,1792]{1,0:T(8,128)(2,1)} custom-call(s32[1]{0:T(128)} %bitcast.7.r_ref, bf16[1792,3584]{1,0:T(8,128)(2,1)} %bitcast.14, bf16[1792,3584]{1,0:T(8,128)(2,1)} %bitcast.15, bf16[672,1792]{1,0:T(8,128)(2,1)} %collective-permute-done.9.near_ref, f32[1792,896]{1,0:T(8,128)} %p_ref.15, f32[1792,896]{1,0:T(8,128)} %m_ref.15), custom_call_target="tpu_custom_call" | custom-call | flops 2000000 | bytes 12042240 | tf_op jit(solution)/shard_map/sums/pallas_call | solution.py:192
  69.9 3.1 %sums.7 = bf16[224,1792]{1,0:T(8,128)(2,1)} custom-call(s32[1]{0:T(128)} %bitcast.7.r_ref, bf16[1792,3584]{1,0:T(8,128)(2,1)} %bitcast.16, bf16[1792,3584]{1,0:T(8,128)(2,1)} %bitcast.17, bf16[224,1792]{1,0:T(8,128)(2,1)} %copy-done.1, f32[1792,896]{1,0:T(8,128)} %p_ref.15, f32[1792,896]{1,0:T(8,128)} %m_ref.15), custom_call_target="tpu_custom_call" | custom-call | flops 2000000 | bytes 4014080 | tf_op jit(solution)/shard_map/sums/pallas_call | solution.py:192
  73.5 2.6 collective-permute-done.3.refs_4_
  76.1 8.3 %join.1 = (bf16[384,3584]{1,0:T(8,128)(2,1)}, bf16[384,3584]{1,0:T(8,128)(2,1)}, bf16[3584,384]{1,0:T(8,128)(2,1)}) custom-call(bf16[96,3584]{1,0:T(8,128)(2,1)} %copy-done.2, bf16[96,3584]{1,0:T(8,128)(2,1)} %collective-permute-done.refs_1_, bf16[96,3584]{1,0:T(8,128)(2,1)} %collective-permute-done.1.refs_2_, ...), custom_call_target="tpu_custom_call" | custom-call | flops 2000000 | bytes 13762560 | tf_op jit(solution)/shard_map/join/pallas_call | solution.py:131
  84.4 23.8 %forward.1 = (bf16[1792,384]{1,0:T(8,128)(2,1)}, bf16[384,1792]{1,0:T(8,128)(2,1)}, bf16[384,1792]{1,0:T(8,128)(2,1)}) custom-call(bf16[384,3584]{1,0:T(8,128)(2,1)} %get-tuple-element.26.x_ref, bf16[384,3584]{1,0:T(8,128)(2,1)} %get-tuple-element.27.c_ref, bf16[3584,1792]{1,0:T(8,128)(2,1)} %bitcast.38, bf16[3584,1792]{1,0:T(8,128)(2,1)} %bitcast.40, ...), custom_call_target="tpu_custom_call" | custom-call | flops 14797504512 | bytes 52297728 | tf_op jit(solution)/shard_map/forward/pallas_call | solution.py:77
  108.2 64.6 %collective-permute-done.14.cross_ref = bf16[224,1792]{1,0:T(8,128)(2,1)S(1)} collective-permute-done((bf16[224,1792]{1,0:T(8,128)(2,1)}, bf16[224,1792]{1,0:T(8,128)(2,1)S(1)}, u32[]{:S(2)}, u32[]{:S(2)}) %collective-permute-start.14) | collective-permute-done | bytes 802848 | tf_op jit(solution)/shard_map/ppermute | solution.py:331
  173.7 3.8 %outer.4 = (f32[1792,896]{1,0:T(8,128)}, f32[1792,896]{1,0:T(8,128)}, bf16[224,1792]{1,0:T(8,128)(2,1)}) custom-call(s32[1]{0:T(128)} %bitcast.7.r_ref, bf16[1792,3584]{1,0:T(8,128)(2,1)} %bitcast.19, bf16[1792,3584]{1,0:T(8,128)(2,1)} %bitcast.20, bf16[224,1792]{1,0:T(8,128)(2,1)} %copy-done.1, bf16[224,1792]{1,0:T(8,128)(2,1)} %copy-done.5, ...), custom_call_target="tpu_custom_call" | custom-call | flops 2000000 | bytes 5619712 | tf_op jit(solution)/shard_map/outer/pallas_call | solution.py:227
  177.5 8.2 %outer.5 = (f32[1792,896]{1,0:T(8,128)}, f32[1792,896]{1,0:T(8,128)}, bf16[672,1792]{1,0:T(8,128)(2,1)}) custom-call(s32[1]{0:T(128)} %bitcast.7.r_ref, bf16[1792,3584]{1,0:T(8,128)(2,1)} %bitcast.21, bf16[1792,3584]{1,0:T(8,128)(2,1)} %bitcast.22, bf16[672,1792]{1,0:T(8,128)(2,1)} %collective-permute-done.11.near_ref, ...), custom_call_target="tpu_custom_call", output_to_operand_aliasing={{0}: (7, {}), {1}: (8, {})} | custom-call | flops 2000000 | bytes 16859136 | tf_op jit(solution)/shard_map/outer/pallas_call | solution.py:227
  185.7 25.6 %update.1 = (bf16[3584,1792]{1,0:T(8,128)(2,1)}, bf16[3584,1792]{1,0:T(8,128)(2,1)}) custom-call(bf16[3584,384]{1,0:T(8,128)(2,1)} %get-tuple-element.25.x_ref, bf16[384,1792]{1,0:T(8,128)(2,1)} %get-tuple-element.28.dg_ref, bf16[384,1792]{1,0:T(8,128)(2,1)} %get-tuple-element.29.du_ref, bf16[3584,1792]{1,0:T(8,128)(2,1)} %bitcast.39, ...), custom_call_target="tpu_custom_call" | custom-call | flops 9865003008 | bytes 51380224 | tf_op jit(solution)/shard_map/update/pallas_call | solution.py:105
  211.3 8.2 %outer.6 = (f32[1792,896]{1,0:T(8,128)}, f32[1792,896]{1,0:T(8,128)}, bf16[672,1792]{1,0:T(8,128)(2,1)}) custom-call(s32[1]{0:T(128)} %bitcast.7.r_ref, bf16[1792,3584]{1,0:T(8,128)(2,1)} %bitcast.23, bf16[1792,3584]{1,0:T(8,128)(2,1)} %bitcast.24, bf16[672,1792]{1,0:T(8,128)(2,1)} %collective-permute-done.9.near_ref, ...), custom_call_target="tpu_custom_call", output_to_operand_aliasing={{0}: (7, {}), {1}: (8, {})} | custom-call | flops 2000000 | bytes 16859136 | tf_op jit(solution)/shard_map/outer/pallas_call | solution.py:227
  220.0 1.9 pack.4
  221.9 3.6 %collective-permute-done.7.near_ref = bf16[224,1792]{1,0:T(8,128)(2,1)S(1)} collective-permute-done((bf16[224,1792]{1,0:T(8,128)(2,1)}, bf16[224,1792]{1,0:T(8,128)(2,1)S(1)}, u32[]{:S(2)}, u32[]{:S(2)}) %collective-permute-start.7) | collective-permute-done | bytes 802848 | tf_op jit(solution)/shard_map/ppermute | solution.py:328
  226.5 3.2 %sums.4 = bf16[224,1792]{1,0:T(8,128)(2,1)} custom-call(s32[1]{0:T(128)} %bitcast.7.r_ref, bf16[1792,3584]{1,0:T(8,128)(2,1)} %bitcast.26, bf16[1792,3584]{1,0:T(8,128)(2,1)} %bitcast.27, bf16[224,1792]{1,0:T(8,128)(2,1)} %copy-done, f32[1792,896]{1,0:T(8,128)} %p_ref.15, f32[1792,896]{1,0:T(8,128)} %m_ref.15), custom_call_target="tpu_custom_call" | custom-call | flops 2000000 | bytes 4014080 | tf_op jit(solution)/shard_map/sums/pallas_call | solution.py:192
  229.6 1.5 collective-permute-start.8
  231.2 18.8 %collective-permute-done.8.cross_ref = bf16[224,1792]{1,0:T(8,128)(2,1)S(1)} collective-permute-done((bf16[224,1792]{1,0:T(8,128)(2,1)}, bf16[224,1792]{1,0:T(8,128)(2,1)S(1)}, u32[]{:S(2)}, u32[]{:S(2)}) %collective-permute-start.8) | collective-permute-done | bytes 802848 | tf_op jit(solution)/shard_map/ppermute | solution.py:331
  250.9 3.9 %outer.7 = (f32[1792,896]{1,0:T(8,128)}, f32[1792,896]{1,0:T(8,128)}, bf16[224,1792]{1,0:T(8,128)(2,1)}) custom-call(s32[1]{0:T(128)} %bitcast.7.r_ref, bf16[1792,3584]{1,0:T(8,128)(2,1)} %bitcast.28, bf16[1792,3584]{1,0:T(8,128)(2,1)} %bitcast.29, bf16[224,1792]{1,0:T(8,128)(2,1)} %copy-done, ...), custom_call_target="tpu_custom_call", output_to_operand_aliasing={{0}: (7, {}), {1}: (8, {})} | custom-call | flops 2000000 | bytes 5619712 | tf_op jit(solution)/shard_map/outer/pallas_call | solution.py:227
  254.8 5.4 %mixed.4.rest_0_ = bf16[1792,3584]{1,0:T(8,128)(2,1)} custom-call(s32[1]{0:T(128)} %bitcast.7.r_ref, bf16[1792,384]{1,0:T(8,128)(2,1)} %get-tuple-element.32.rest_0_.rest_2_.h_ref, bf16[384,3584]{1,0:T(8,128)(2,1)} %get-tuple-element.27.c_ref, bf16[1792,3584]{1,0:T(8,128)(2,1)} %bitcast.30, bf16[224,1792]{1,0:T(8,128)(2,1)} %get-tuple-element.42.mine_ref, ...), custom_call_target="tpu_custom_call" | custom-call | flops 616562688 | bytes 4816896 | tf_op jit(solution)/shard_map/mixed/pallas_call | solution.py:263
  260.2 12.9 %mixed.5.rest_0_ = bf16[1792,3584]{1,0:T(8,128)(2,1)} custom-call(s32[1]{0:T(128)} %bitcast.7.r_ref, bf16[1792,384]{1,0:T(8,128)(2,1)} %get-tuple-element.32.rest_0_.rest_2_.h_ref, bf16[384,3584]{1,0:T(8,128)(2,1)} %get-tuple-element.27.c_ref, bf16[1792,3584]{1,0:T(8,128)(2,1)} %bitcast.31, ...), custom_call_target="tpu_custom_call", output_to_operand_aliasing={{}: (6, {})} | custom-call | flops 1849688064 | bytes 14450688 | tf_op jit(solution)/shard_map/mixed/pallas_call | solution.py:263
  273.0 12.9 %mixed.6.rest_0_ = bf16[1792,3584]{1,0:T(8,128)(2,1)} custom-call(s32[1]{0:T(128)} %bitcast.7.r_ref, bf16[1792,384]{1,0:T(8,128)(2,1)} %get-tuple-element.32.rest_0_.rest_2_.h_ref, bf16[384,3584]{1,0:T(8,128)(2,1)} %get-tuple-element.27.c_ref, bf16[1792,3584]{1,0:T(8,128)(2,1)} %bitcast.32, ...), custom_call_target="tpu_custom_call", output_to_operand_aliasing={{}: (6, {})} | custom-call | flops 1849688064 | bytes 14450688 | tf_op jit(solution)/shard_map/mixed/pallas_call | solution.py:263
  286.8 5.4 %mixed.7 = bf16[1792,3584]{1,0:T(8,128)(2,1)} custom-call(s32[1]{0:T(128)} %bitcast.7.r_ref, bf16[1792,384]{1,0:T(8,128)(2,1)} %get-tuple-element.32.rest_0_.rest_2_.h_ref, bf16[384,3584]{1,0:T(8,128)(2,1)} %get-tuple-element.27.c_ref, bf16[1792,3584]{1,0:T(8,128)(2,1)} %bitcast.33, ...), custom_call_target="tpu_custom_call", output_to_operand_aliasing={{}: (6, {})} | custom-call | flops 616562688 | bytes 4816896 | tf_op jit(solution)/shard_map/mixed/pallas_call | solution.py:263
  (40 shorter events, 11.3 us)
Async XLA Ops:
  0.6 5.5 %copy-start.6 = (bf16[1,48,3584]{2,1,0:T(8,128)(2,1)S(1)}, bf16[1,48,3584]{2,1,0:T(8,128)(2,1)}, u32[]{:S(2)}) copy-start(bf16[1,48,3584]{2,1,0:T(8,128)(2,1)} %param.8) | copy-start | bytes 1032196
  5.7 39.4 %collective-permute-start.11 = (bf16[672,1792]{1,0:T(8,128)(2,1)}, bf16[672,1792]{1,0:T(8,128)(2,1)}, u32[]{:S(2)}, u32[]{:S(2)}) collective-permute-start(bf16[672,1792]{1,0:T(8,128)(2,1)} %pack.6), channel_id=1, source_target_pairs={{0,8},{8,0},{16,24},{24,16},{1,9},{9,1},{17,25},{25,17},{2,10},{10... | collective-permute-start | bytes 7225352 | tf_op jit(solution)/shard_map/ppermute | solution.py:328
  7.2 7.8 %copy-start.2 = (bf16[96,3584]{1,0:T(8,128)(2,1)}, bf16[96,3584]{1,0:T(8,128)(2,1)S(1)}, u32[]{:S(2)}) copy-start(bf16[96,3584]{1,0:T(8,128)(2,1)S(1)} %pad_maximum_fusion.refs_0_) | copy-start | bytes 2064388
  7.2 18.8 %collective-permute-start = (bf16[96,3584]{1,0:T(8,128)(2,1)S(1)}, bf16[96,3584]{1,0:T(8,128)(2,1)}, u32[]{:S(2)}, u32[]{:S(2)}) collective-permute-start(bf16[96,3584]{1,0:T(8,128)(2,1)S(1)} %pad_maximum_fusion.refs_0_), channel_id=1, source_target_pairs={{0,2},{2,4},{4,6},{6,7},{7,5},{5,3},{3,1},{1,0},{8,10},{10,12},{12... | collective-permute-start | bytes 2064392 | tf_op jit(solution)/shard_map/ppermute | solution.py:321
  14.7 46.8 %collective-permute-start.9 = (bf16[672,1792]{1,0:T(8,128)(2,1)}, bf16[672,1792]{1,0:T(8,128)(2,1)}, u32[]{:S(2)}, u32[]{:S(2)}) collective-permute-start(bf16[672,1792]{1,0:T(8,128)(2,1)} %pack.5), channel_id=1, source_target_pairs={{0,8},{8,0},{16,24},{24,16},{1,9},{9,1},{17,25},{25,17},{2,10},{10... | collective-permute-start | bytes 7225352 | tf_op jit(solution)/shard_map/ppermute | solution.py:328
  15.0 17.7 %collective-permute-start.4 = (bf16[96,3584]{1,0:T(8,128)(2,1)S(1)}, bf16[96,3584]{1,0:T(8,128)(2,1)}, u32[]{:S(2)}, u32[]{:S(2)}) collective-permute-start(bf16[96,3584]{1,0:T(8,128)(2,1)S(1)} %pad_maximum_fusion.refs_0_), channel_id=1, source_target_pairs={{2,0},{4,2},{6,4},{7,6},{5,7},{3,5},{1,3},{0,1},{10,8},{12,10},{14... | collective-permute-start | bytes 2064392 | tf_op jit(solution)/shard_map/ppermute | solution.py:323
  26.0 17.6 %collective-permute-start.1 = (bf16[96,3584]{1,0:T(8,128)(2,1)}, bf16[96,3584]{1,0:T(8,128)(2,1)}, u32[]{:S(2)}, u32[]{:S(2)}) collective-permute-start(bf16[96,3584]{1,0:T(8,128)(2,1)} %collective-permute-done.refs_1_), channel_id=1, source_target_pairs={{0,2},{2,4},{4,6},{6,7},{7,5},{5,3},{3,1},{1,0},{8,10},{10,12},{12... | collective-permute-start | bytes 2064392 | tf_op jit(solution)/shard_map/ppermute | solution.py:321
  32.7 21.8 %collective-permute-start.5 = (bf16[96,3584]{1,0:T(8,128)(2,1)}, bf16[96,3584]{1,0:T(8,128)(2,1)}, u32[]{:S(2)}, u32[]{:S(2)}) collective-permute-start(bf16[96,3584]{1,0:T(8,128)(2,1)} %collective-permute-done.4.refs_7_), channel_id=1, source_target_pairs={{2,0},{4,2},{6,4},{7,6},{5,7},{3,5},{1,3},{0,1},{10,8},{12,10},{14... | collective-permute-start | bytes 2064392 | tf_op jit(solution)/shard_map/ppermute | solution.py:323
  43.5 16.7 %collective-permute-start.2 = (bf16[96,3584]{1,0:T(8,128)(2,1)}, bf16[96,3584]{1,0:T(8,128)(2,1)}, u32[]{:S(2)}, u32[]{:S(2)}) collective-permute-start(bf16[96,3584]{1,0:T(8,128)(2,1)} %collective-permute-done.1.refs_2_), channel_id=1, source_target_pairs={{0,2},{2,4},{4,6},{6,7},{7,5},{5,3},{3,1},{1,0},{8,10},{10,12},{12... | collective-permute-start | bytes 2064392 | tf_op jit(solution)/shard_map/ppermute | solution.py:321
  51.1 126.5 %collective-permute-start.12 = (bf16[672,1792]{1,0:T(8,128)(2,1)}, bf16[672,1792]{1,0:T(8,128)(2,1)}, u32[]{:S(2)}, u32[]{:S(2)}) collective-permute-start(bf16[672,1792]{1,0:T(8,128)(2,1)} %sums.6), channel_id=1, source_target_pairs={{0,16},{8,24},{16,0},{24,8},{1,17},{9,25},{17,1},{25,9},{2,18},{10... | collective-permute-start | bytes 7225352 | tf_op jit(solution)/shard_map/ppermute | solution.py:331
  54.5 14.6 %collective-permute-start.13 = (bf16[224,1792]{1,0:T(8,128)(2,1)}, bf16[224,1792]{1,0:T(8,128)(2,1)S(1)}, u32[]{:S(2)}, u32[]{:S(2)}) collective-permute-start(bf16[224,1792]{1,0:T(8,128)(2,1)} %pack.7), channel_id=1, source_target_pairs={{0,8},{8,0},{16,24},{24,16},{1,9},{9,1},{17,25},{25,17},{2,10},{10... | collective-permute-start | bytes 2408456 | tf_op jit(solution)/shard_map/ppermute | solution.py:328
  54.5 19.0 %collective-permute-start.6 = (bf16[96,3584]{1,0:T(8,128)(2,1)}, bf16[96,3584]{1,0:T(8,128)(2,1)}, u32[]{:S(2)}, u32[]{:S(2)}) collective-permute-start(bf16[96,3584]{1,0:T(8,128)(2,1)} %collective-permute-done.5.refs_6_), channel_id=1, source_target_pairs={{2,0},{4,2},{6,4},{7,6},{5,7},{3,5},{1,3},{0,1},{10,8},{12,10},{14... | collective-permute-start | bytes 2064392 | tf_op jit(solution)/shard_map/ppermute | solution.py:323
  60.3 15.9 %collective-permute-start.3 = (bf16[96,3584]{1,0:T(8,128)(2,1)}, bf16[96,3584]{1,0:T(8,128)(2,1)}, u32[]{:S(2)}, u32[]{:S(2)}) collective-permute-start(bf16[96,3584]{1,0:T(8,128)(2,1)} %collective-permute-done.2.refs_3_), channel_id=1, source_target_pairs={{0,2},{2,4},{4,6},{6,7},{7,5},{5,3},{3,1},{1,0},{8,10},{10,12},{12... | collective-permute-start | bytes 2064392 | tf_op jit(solution)/shard_map/ppermute | solution.py:321
  67.5 143.8 %collective-permute-start.10 = (bf16[672,1792]{1,0:T(8,128)(2,1)}, bf16[672,1792]{1,0:T(8,128)(2,1)}, u32[]{:S(2)}, u32[]{:S(2)}) collective-permute-start(bf16[672,1792]{1,0:T(8,128)(2,1)} %sums.5), channel_id=1, source_target_pairs={{0,16},{8,24},{16,0},{24,8},{1,17},{9,25},{17,1},{25,9},{2,18},{10... | collective-permute-start | bytes 7225352 | tf_op jit(solution)/shard_map/ppermute | solution.py:331
  69.0 0.9 copy-start.1
  73.0 99.8 %collective-permute-start.14 = (bf16[224,1792]{1,0:T(8,128)(2,1)}, bf16[224,1792]{1,0:T(8,128)(2,1)S(1)}, u32[]{:S(2)}, u32[]{:S(2)}) collective-permute-start(bf16[224,1792]{1,0:T(8,128)(2,1)} %sums.7), channel_id=1, source_target_pairs={{0,16},{8,24},{16,0},{24,8},{1,17},{9,25},{17,1},{25,9},{2,18},{10... | collective-permute-start | bytes 2408456 | tf_op jit(solution)/shard_map/ppermute | solution.py:331
  172.8 0.9 copy-start.5
  185.7 74.5 %collective-permute-start.17 = (bf16[672,1792]{1,0:T(8,128)(2,1)}, bf16[672,1792]{1,0:T(8,128)(2,1)}, u32[]{:S(2)}, u32[]{:S(2)}) collective-permute-start(bf16[672,1792]{1,0:T(8,128)(2,1)} %get-tuple-element.41.mine_ref), channel_id=1, source_target_pairs={{0,8},{8,0},{16,24},{24,16},{1,9},{9,1},{17,25},{25,17},{2,10},{10... | collective-permute-start | bytes 7225352 | tf_op jit(solution)/shard_map/ppermute | solution.py:347
  219.5 53.5 %collective-permute-start.16 = (bf16[672,1792]{1,0:T(8,128)(2,1)}, bf16[672,1792]{1,0:T(8,128)(2,1)}, u32[]{:S(2)}, u32[]{:S(2)}) collective-permute-start(bf16[672,1792]{1,0:T(8,128)(2,1)} %get-tuple-element.40.mine_ref), channel_id=1, source_target_pairs={{0,8},{8,0},{16,24},{24,16},{1,9},{9,1},{17,25},{25,17},{2,10},{10... | collective-permute-start | bytes 7225352 | tf_op jit(solution)/shard_map/ppermute | solution.py:347
  221.9 3.7 %collective-permute-start.7 = (bf16[224,1792]{1,0:T(8,128)(2,1)}, bf16[224,1792]{1,0:T(8,128)(2,1)S(1)}, u32[]{:S(2)}, u32[]{:S(2)}) collective-permute-start(bf16[224,1792]{1,0:T(8,128)(2,1)} %pack.4), channel_id=1, source_target_pairs={{0,8},{8,0},{16,24},{24,16},{1,9},{9,1},{17,25},{25,17},{2,10},{10... | collective-permute-start | bytes 2408456 | tf_op jit(solution)/shard_map/ppermute | solution.py:328
  225.6 0.9 copy-start
  229.6 20.4 %collective-permute-start.8 = (bf16[224,1792]{1,0:T(8,128)(2,1)}, bf16[224,1792]{1,0:T(8,128)(2,1)S(1)}, u32[]{:S(2)}, u32[]{:S(2)}) collective-permute-start(bf16[224,1792]{1,0:T(8,128)(2,1)} %sums.4), channel_id=1, source_target_pairs={{0,16},{8,24},{16,0},{24,8},{1,17},{9,25},{17,1},{25,9},{2,18},{10... | collective-permute-start | bytes 2408456 | tf_op jit(solution)/shard_map/ppermute | solution.py:331
  231.1 23.6 %collective-permute-start.18 = (bf16[224,1792]{1,0:T(8,128)(2,1)}, bf16[224,1792]{1,0:T(8,128)(2,1)}, u32[]{:S(2)}, u32[]{:S(2)}) collective-permute-start(bf16[224,1792]{1,0:T(8,128)(2,1)} %get-tuple-element.42.mine_ref), channel_id=1, source_target_pairs={{0,8},{8,0},{16,24},{24,16},{1,9},{9,1},{17,25},{25,17},{2,10},{10... | collective-permute-start | bytes 2408456 | tf_op jit(solution)/shard_map/ppermute | solution.py:347
  250.0 0.9 copy-start.4
  254.8 31.1 %collective-permute-start.15 = (bf16[224,1792]{1,0:T(8,128)(2,1)}, bf16[224,1792]{1,0:T(8,128)(2,1)S(1)}, u32[]{:S(2)}, u32[]{:S(2)}) collective-permute-start(bf16[224,1792]{1,0:T(8,128)(2,1)} %get-tuple-element.39.mine_ref), channel_id=1, source_target_pairs={{0,8},{8,0},{16,24},{24,16},{1,9},{9,1},{17,25},{25,17},{2,10},{10... | collective-permute-start | bytes 2408456 | tf_op jit(solution)/shard_map/ppermute | solution.py:347
  285.9 0.9 copy-start.3
